TPU v7x, 512 devices: a 8x2x16 block of a 8x16x16 slice. The times are simulated.
512 devices in a mesh: groups: 2 (over y), seq: 32 (over z, core), rep: 8 (over x).
Axes of the slice: x: 8, y: 2, z: 16, core: 2. Of those that a mesh axis runs over, the one named last changes fastest.
The devices are a block of a 8x16x16 slice.
Arguments:
- queries: bfloat16 [1024, 4096], P(('groups', 'seq'), 'rep'), parts along dimension 0, may hold values from -128 to 128
- keys_new: bfloat16 [1024, 1024], P(('groups', 'seq'), 'rep'), parts along dimension 0, may hold values from -4 to 4
- values_new: bfloat16 [1024, 1024], P(('groups', 'seq'), 'rep'), parts along dimension 0, may hold values from -6 to 6
- keys_past: bfloat16 [16384, 1024], P(('groups', 'seq'), 'rep'), parts along dimension 0, may hold values from -4 to 4
- values_past: bfloat16 [16384, 1024], P(('groups', 'seq'), 'rep'), parts along dimension 0, may hold values from -6 to 6
- block_order: int32 [64], P('groups'), parts along dimension 0, may hold values from 0 to 31, each once
- residual: bfloat16 [1024, 4096], P(('groups', 'seq'), 'rep'), parts along dimension 0, may hold values from -6 to 6
- out_proj: bfloat16 [4096, 4096], P('seq', 'rep'), may hold values from -0.09375 to 0.09375
- norm_gain: float32 [4096], replicated, may hold values from 0.5 to 1.5
- router: float32 [4096, 4], replicated, may hold values from -0.09375 to 0.09375
- w_gate: bfloat16 [8, 4096, 4096], P('rep', None, 'seq'), may hold values from -0.09375 to 0.09375
- w_up: bfloat16 [8, 4096, 4096], P('rep', None, 'seq'), may hold values from -0.09375 to 0.09375
- w_down: bfloat16 [8, 4096, 4096], P('rep', 'seq'), may hold values from -0.0625 to 0.0625
- expert_ids: int32 [1024, 2], P(('groups', 'seq')), parts along dimension 0, may hold values from 0 to 3, all different within a row; in each aligned block of 16 rows (0 to 15, 16 to 31, ...) at most 12 rows name the same one
Outputs:
- attended: bfloat16 [1024, 4096], P(('groups', 'seq'), 'rep'), parts along dimension 0
- layer_out: bfloat16 [1024, 4096], P(('groups', 'seq'), 'rep'), parts along dimension 0
- keys_cache: bfloat16 [1024, 1024], P(('groups', 'seq')), parts along dimension 0
- values_cache: bfloat16 [1024, 1024], P(('groups', 'seq')), parts along dimension 0
There are 2 independent parts, one for each index of `groups`. A program takes and returns all parts, laid end to end along the dimension named above; an argument that names none is the same for every part. Nothing has to cross between parts.
Inputs may be any that keep to these rules, and one draw needn't show every extreme that they name: `block_order`: each block index 0 to 32 - 1 appears once. `expert_ids`: each row names 2 different experts; in the rows of one device (aligned blocks of 16 rows) no expert is named by more than 12 rows, and in some block one expert is named by exactly 12.
All inputs are finite; a program needn't handle non-finite values.
Results may differ from a plain program's by a relative error of at most 0.011.
Values may be sent and summed in bfloat16 or wider, within the bound.
A program may use at most 64 MiB of HBM per device.

v0:
```python
import math
import jax
import jax.numpy as jnp
from jax import lax
from jax.sharding import Mesh
from jax.sharding import PartitionSpec as P

EXPERTS = 4
CAP = 12
SEQ = ("seq_0", "seq_1")
GROUPS_SEQ = ("groups", "seq_0", "seq_1")


def in_one_piece(arrays, axis, dim, along):
    both = jnp.concatenate(arrays, axis=along)
    out, at, gathered = (lax.all_gather(both, axis, axis=dim, tiled=True), 0, [])
    for a in arrays:
        gathered.append(lax.slice_in_dim(out, at, at + a.shape[along], axis=along))
        at += a.shape[along]
    return tuple(gathered)


def sent_to_all(array, axis):
    size = lax.axis_size(axis)
    return lax.all_to_all(
        jnp.broadcast_to(array[None], (size, *array.shape)), axis, 0, 0, tiled=True
    )


def laid_out(tiles, dim):
    tiles = jnp.moveaxis(tiles, 0, dim)
    shape = tiles.shape
    return tiles.reshape(*shape[:dim], shape[dim] * shape[dim + 1], *shape[dim + 2 :])


def gather_directly(array, axis, dim):
    tiles = sent_to_all(array, axis)
    return laid_out(tiles, dim)


def own_block(tiles, axes, order):
    shape = [lax.axis_size(a) for a in axes]
    tiles = tiles.reshape(*shape, *tiles.shape[1:])
    tiles = tiles.transpose(*order, *range(len(axes), tiles.ndim))
    tiles = tiles.reshape(-1, *tiles.shape[len(axes) :])
    for k in order:
        tiles = lax.psum_scatter(tiles, axes[k], scatter_dimension=0, tiled=True)
    return tiles[0]


def in_blocks(array, dim, size):
    shape = array.shape
    tiles = array.reshape(*shape[:dim], size, shape[dim] // size, *shape[dim + 1 :])
    return jnp.moveaxis(tiles, dim, 0)


def sum_by_axis(array, axes, order, dim):
    size = lax.axis_size(axes)
    return own_block(in_blocks(array, dim, size), axes, order)


def block_lookup(owners, block_order):
    width = block_order.shape[0]
    hits = owners[:, None] == jnp.arange(width, dtype=jnp.int32)[None, :]
    return jnp.sum(jnp.where(hits, block_order[None, :], 0), axis=1)


def body(
    queries,
    keys_new,
    values_new,
    keys_past,
    values_past,
    block_order,
    residual,
    out_proj,
    norm_gain,
    router,
    w_gate,
    w_up,
    w_down,
    expert_ids,
):
    seq_index = lax.axis_index(SEQ)
    rep_index = lax.axis_index("rep")
    rep_count = lax.axis_size("rep")
    tok_count = queries.shape[0]
    head_dim = keys_new.shape[1]
    q_per = queries.shape[1] // head_dim
    past_len = keys_past.shape[0]
    key_span = past_len + tok_count
    row_total = tok_count * q_per
    my_block = block_lookup(jnp.full((1,), seq_index, jnp.int32), block_order)[0]
    scaling = 1.0 / math.sqrt(head_dim)
    query_rows = queries.reshape(row_total, head_dim)
    query_pos = my_block * tok_count + jnp.arange(row_total, dtype=jnp.int32) // q_per
    keys_local = jnp.concatenate([keys_past, keys_new], axis=0)
    values_local = jnp.concatenate([values_past, values_new], axis=0)
    running = jnp.full((row_total,), -1e30, jnp.float32)
    key_piece, value_piece = in_one_piece((keys_local, values_local), SEQ, 0, 1)
    row_count = key_piece.shape[0]
    key_index = jnp.arange(row_count, dtype=jnp.int32)
    key_owner = key_index // key_span
    offset = key_index % key_span
    key_pos = block_lookup(key_owner, block_order) * tok_count + offset - past_len
    visible = (offset < past_len)[None, :] | (key_pos[None, :] <= query_pos[:, None])
    scores = jnp.dot(query_rows, key_piece.T, preferred_element_type=jnp.float32) * scaling
    highest = jnp.maximum(running, jnp.max(jnp.where(visible, scores, -1e30), axis=1))
    weights = jnp.where(visible, jnp.exp(scores - highest[:, None]), 0.0)
    totals = jnp.sum(weights, axis=1)
    numerator = jnp.dot(
        weights.astype(jnp.bfloat16), value_piece, preferred_element_type=jnp.float32
    )
    running, totals, numerator = (highest, totals, numerator)
    attn_local = (
        (numerator / totals[:, None]).reshape(tok_count, q_per * head_dim).astype(jnp.bfloat16)
    )
    attn_full, keys_cache, values_cache = (
        lax.all_gather(attn_local, "rep", axis=1, tiled=True),
        *in_one_piece((keys_new, values_new), "rep", 1, 0),
    )
    projected = jnp.dot(
        attn_full,
        lax.all_gather(out_proj, SEQ, axis=0, tiled=True),
        preferred_element_type=jnp.float32,
    )
    attended = (residual.astype(jnp.float32) + projected).astype(jnp.bfloat16)
    full_rows = gather_directly(attended, "rep", 1)
    features = full_rows.astype(jnp.float32)
    mean_square = jnp.mean(features * features, axis=1, keepdims=True)
    normed = (features * norm_gain[None, :] * lax.rsqrt(mean_square + 1e-05)).astype(jnp.bfloat16)
    logits = jnp.dot(normed.astype(jnp.float32), router, precision=lax.Precision.HIGHEST)
    expert_range = jnp.arange(EXPERTS, dtype=jnp.int32)
    first_pick = (expert_ids[:, 0:1] == expert_range[None, :]).astype(jnp.float32)
    second_pick = (expert_ids[:, 1:2] == expert_range[None, :]).astype(jnp.float32)
    share_first = jax.nn.sigmoid(
        jnp.sum(first_pick * logits, axis=1) - jnp.sum(second_pick * logits, axis=1)
    )
    token_share = share_first[:, None] * first_pick + (1.0 - share_first)[:, None] * second_pick
    member = first_pick + second_pick
    ranking = jnp.cumsum(member, axis=0) - member
    slot_range = jnp.arange(CAP, dtype=jnp.float32)
    selection = member.T[:, None, :] * (ranking.T[:, None, :] == slot_range[None, :, None]).astype(
        jnp.float32
    )
    mine_mask = (expert_range == rep_index % EXPERTS).astype(jnp.float32)
    my_selection = jnp.einsum("e,ejt->jt", mine_mask, selection)
    slot_rows = jnp.dot(
        my_selection.astype(jnp.bfloat16), normed, preferred_element_type=jnp.float32
    ).astype(jnp.bfloat16)
    gate_local = w_gate[0]
    up_local = w_up[0]
    down_local = w_down[0]
    piece = lax.all_gather(slot_rows, SEQ, axis=0, tiled=True)
    gate_part = jnp.dot(piece, gate_local, preferred_element_type=jnp.float32)
    up_part = jnp.dot(piece, up_local, preferred_element_type=jnp.float32)
    hidden_slots = (jax.nn.silu(gate_part) * up_part).astype(jnp.bfloat16)
    expert_part = sum_by_axis(
        jnp.dot(hidden_slots, down_local, preferred_element_type=jnp.float32).astype(jnp.bfloat16),
        SEQ,
        (1, 0),
        0,
    ).astype(jnp.float32)
    returned = lax.all_to_all(
        expert_part.astype(jnp.bfloat16), "rep", split_axis=1, concat_axis=0, tiled=True
    ).astype(expert_part.dtype)
    source_expert = jnp.arange(rep_count, dtype=jnp.int32) % EXPERTS
    source_pick = (source_expert[:, None] == expert_range[None, :]).astype(jnp.float32)
    combine = jnp.einsum("re,ejt,te->trj", source_pick, selection, token_share).reshape(
        tok_count, rep_count * CAP
    )
    moe_slice = jnp.dot(combine, returned, precision=lax.Precision.HIGHEST)
    layer_out = (attended.astype(jnp.float32) + moe_slice).astype(jnp.bfloat16)
    return (attended, layer_out, keys_cache, values_cache)


def solution(mesh):
    split = Mesh(
        mesh.devices.reshape(mesh.shape["groups"], 16, 2, mesh.shape["rep"]),
        ("groups", "seq_0", "seq_1", "rep"),
    )
    return jax.shard_map(
        body,
        mesh=split,
        in_specs=(
            P(GROUPS_SEQ, "rep"),
            P(GROUPS_SEQ, "rep"),
            P(GROUPS_SEQ, "rep"),
            P(GROUPS_SEQ, "rep"),
            P(GROUPS_SEQ, "rep"),
            P("groups"),
            P(GROUPS_SEQ, "rep"),
            P(SEQ, "rep"),
            P(),
            P(),
            P("rep", None, SEQ),
            P("rep", None, SEQ),
            P("rep", SEQ, None),
            P(GROUPS_SEQ, None),
        ),
        out_specs=(
            P(GROUPS_SEQ, "rep"),
            P(GROUPS_SEQ, "rep"),
            P(GROUPS_SEQ, None),
            P(GROUPS_SEQ, None),
        ),
        check_vma=False,
    )
```

profile of v0, /device:TPU:66, one launch (start us, length us, event | category | flops | bytes accessed | tf_op | source)
XLA Modules:
  0.0 435.2 jit_solution(9324647808169427397)
XLA Ops:
  7.2 0.0 copy-start
  7.2 0.1 all-gather.5.cloned.1.call-start
  7.3 1.7 maximum_maximum_fusion
  8.9 0.1 all-gather.5.cloned.1.call-update
  9.0 0.1 all-gather.7.cloned.1.call-start
  9.0 0.7 all-gather.7.cloned.1.call-update
  9.8 0.7 reshape.156
  10.5 1.3 fusion.64
  12.5 0.9 select_reduce_fusion.1
  13.5 106.4 %all-gather.5.cloned.1.call-done = bf16[8704,256]{1,0:T(8,128)(2,1)} async-done(((bf16[272,256]{1,0:T(8,128)(2,1)}), bf16[8704,256]{1,0:T(8,128)(2,1)}) %all-gather.5.cloned.1.call-update) | async-done | bytes 4456464 | tf_op jit(solution)/shard_map/all_gather | solution.py:16
  119.9 2.8 select_reduce_fusion
  122.7 0.9 fusion.5
  123.6 0.0 copy-start.6
  123.6 0.8 fusion.22
  124.5 24.7 %all_gather.16 = bf16[16,4096]{1,0:T(8,128)(2,1)S(1)} all-gather(bf16[16,512]{1,0:T(8,128)(2,1)S(1)} %convert_element_type.81), channel_id=1, replica_groups=mesh['groups'=2,'seq_0'=16,'seq_1'=2,'rep'=8] {'rep'}, dimensions={1}, use_global_device_ids=true | all-gather | bytes 147456 | tf_op jit(solution)/shard_map/all_gather | solution.py:119
  149.2 44.8 %all-gather.7.cloned.1.call-done = bf16[4096,512]{1,0:T(8,128)(2,1)} async-done(((bf16[128,512]{1,0:T(8,128)(2,1)}), bf16[4096,512]{1,0:T(8,128)(2,1)}) %all-gather.7.cloned.1.call-update) | async-done | bytes 4194320 | tf_op jit(solution)/shard_map/all_gather | solution.py:124
  194.0 2.8 fusion.16
  196.8 0.7 broadcast_in_dim.33
  197.5 7.2 %all-to-all-start = ((bf16[8,16,512]{2,1,0:T(8,128)(2,1)}), bf16[8,16,512]{2,1,0:T(8,128)(2,1)S(1)}, u32[]{:S(2)}, u32[]{:S(2)}) async-start(bf16[8,16,512]{2,1,0:T(8,128)(2,1)} %broadcast_in_dim.33), calls=%async_computation | async-start | bytes 262144 | tf_op jit(solution)/shard_map/all_to_all | solution.py:25
  204.8 8.0 %all-to-all-done = bf16[8,16,512]{2,1,0:T(8,128)(2,1)S(1)} async-done(((bf16[8,16,512]{2,1,0:T(8,128)(2,1)}), bf16[8,16,512]{2,1,0:T(8,128)(2,1)S(1)}, u32[]{:S(2)}, u32[]{:S(2)}) %all-to-all-start) | async-done | bytes 131104 | tf_op jit(solution)/shard_map/all_to_all | solution.py:25
  212.8 0.1 fusion.32
  213.0 0.3 select_reduce_fusion.2
  213.3 0.1 copy.48
  213.5 0.1 copy.49
  213.5 0.1 fusion.47
  213.7 0.9 fusion.1
  214.6 0.1 all-gather.9.cloned.1.call-update
  214.6 0.1 reduce-scatter.3.cloned.1.call-start
  214.7 68.2 %all-gather.9.cloned.1.call-done = bf16[32,12,4096]{2,1,0:T(8,128)(2,1)} async-done(((bf16[1,12,4096]{2,1,0:T(8,128)(2,1)}), bf16[32,12,4096]{2,1,0:T(8,128)(2,1)}) %all-gather.9.cloned.1.call-update) | async-done | bytes 3145744 | tf_op jit(solution)/shard_map/all_gather | solution.py:154
  282.9 5.6 %reshape.160 = bf16[384,4096]{1,0:T(8,128)(2,1)} reshape(bf16[32,12,4096]{2,1,0:T(8,128)(2,1)} %all-gather.9.cloned.1.call-done) | data formatting | bytes 6291456
  288.5 2.9 fusion.30
  291.5 7.0 %convolution_convert_fusion = bf16[384,4096]{1,0:T(8,128)(2,1)} fusion(bf16[384,4096]{1,0:T(8,128)(2,1)} %reshape.160, bf16[1,128,4096]{2,1,0:T(8,128)(2,1)S(1)} %copy-done, bf16[1,4096,128]{2,1,0:T(8,128)(2,1)S(1)} %copy-done.2, f32[384,128]{1,0:T(8,128)S(1)} %fusion.30), kind=kOutput, calls=%fused_computation.2 | convolution fusion | flops 807174144 | bytes 8585216 | tf_op jit(solution)/shard_map/dot_general | solution.py:159
  298.5 5.5 %reshape_reshape.3 = bf16[16,2,12,4096]{3,2,1,0:T(8,128)(2,1)} reshape(bf16[384,4096]{1,0:T(8,128)(2,1)} %convolution_convert_fusion) | data formatting | bytes 6291456 | tf_op jit(solution)/shard_map/reshape;reshape | solution.py:43
  304.0 5.6 %copy.51 = bf16[2,16,12,4096]{3,1,0,2:T(8,128)(2,1)} copy(bf16[2,16,12,4096]{3,2,0,1:T(8,128)(2,1)} %bitcast.62) | data formatting | bytes 6291456 | tf_op jit(solution)/shard_map/transpose | solution.py:44
  309.6 0.1 reduce-scatter.3.cloned.1.call-update
  309.7 0.2 reduce-scatter.5.cloned.1.call-start
  309.9 19.5 %reduce-scatter.3.cloned.1.call-done = bf16[16,12,4096]{2,0,1:T(8,128)(2,1)} async-done(((bf16[32,12,4096]{2,0,1:T(8,128)(2,1)}), bf16[16,12,4096]{2,0,1:T(8,128)(2,1)}) %reduce-scatter.3.cloned.1.call-update) | async-done | bytes 1572880 | tf_op jit(solution)/shard_map/reduce_scatter | solution.py:47
  329.5 3.7 copy.52
  333.1 0.1 reduce-scatter.5.cloned.1.call-update
  333.2 22.3 %all_gather.19 = bf16[32,1024]{1,0:T(8,128)(2,1)S(1)} all-gather(bf16[32,128]{1,0:T(8,128)(2,1)S(1)} %pad_maximum_fusion), channel_id=1, replica_groups=mesh['groups'=2,'seq_0'=16,'seq_1'=2,'rep'=8] {'rep'}, dimensions={1}, use_global_device_ids=true | all-gather | bytes 73728 | tf_op jit(solution)/shard_map/all_gather | solution.py:16
  355.6 0.6 fusion.72
  356.2 54.9 %reduce-scatter.5.cloned.1.call-done = bf16[1,12,4096]{2,1,0:T(8,128)(2,1)} async-done(((bf16[16,12,4096]{2,1,0:T(8,128)(2,1)}), bf16[1,12,4096]{2,1,0:T(8,128)(2,1)}) %reduce-scatter.5.cloned.1.call-update) | async-done | bytes 98320 | tf_op jit(solution)/shard_map/reduce_scatter | solution.py:47
  411.1 0.9 copy.57
  412.0 0.7 copy.53
  412.7 7.4 %all-to-all-start.1 = ((bf16[12,8,512]{2,0,1:T(8,128)(2,1)}), bf16[12,8,512]{2,0,1:T(8,128)(2,1)S(1)}, u32[]{:S(2)}, u32[]{:S(2)}) async-start(bf16[12,8,512]{2,0,1:T(8,128)(2,1)} %copy.53), calls=%async_computation.3 | async-start | bytes 262144 | tf_op jit(solution)/shard_map/all_to_all | solution.py:164
  420.2 0.2 convolution_bitcast_fusion
  420.4 7.4 %all-to-all-done.1 = bf16[12,8,512]{2,0,1:T(8,128)(2,1)S(1)} async-done(((bf16[12,8,512]{2,0,1:T(8,128)(2,1)}), bf16[12,8,512]{2,0,1:T(8,128)(2,1)S(1)}, u32[]{:S(2)}, u32[]{:S(2)}) %all-to-all-start.1) | async-done | bytes 98336 | tf_op jit(solution)/shard_map/all_to_all | solution.py:164
  427.8 0.8 fusion.15
  (38 shorter events, 0.3 us)
Async XLA Ops:
  7.2 284.3 %copy-start = (bf16[1,128,4096]{2,1,0:T(8,128)(2,1)S(1)}, bf16[1,128,4096]{2,1,0:T(8,128)(2,1)}, u32[]{:S(2)}) copy-start(bf16[1,128,4096]{2,1,0:T(8,128)(2,1)} %param.26) | copy-start | bytes 3145732
  7.2 112.7 %all-gather.5.cloned.1.call-start = ((), (), s32[]{:S(2)}) async-start(), calls=%async_computation.4 | async-start | bytes 4595712 | tf_op jit(solution)/shard_map/all_gather | solution.py:16
  9.0 185.0 %all-gather.7.cloned.1.call-start = ((), (), s32[]{:S(2)}) async-start(), calls=%async_computation.5 | async-start | bytes 4325376 | tf_op jit(solution)/shard_map/all_gather | solution.py:124
  119.9 3.7 copy-start.10
  123.6 70.4 %copy-start.6 = (bf16[16,512]{1,0:T(8,128)(2,1)S(1)}, bf16[16,512]{1,0:T(8,128)(2,1)}, u32[]{:S(2)}) copy-start(bf16[16,512]{1,0:T(8,128)(2,1)} %param.20) | copy-start | bytes 49156
  149.2 55.5 %copy-start.9 = (s32[16,2]{0,1:T(2,128)S(1)}, s32[16,2]{0,1:T(2,128)}, u32[]{:S(2)}) copy-start(s32[16,2]{0,1:T(2,128)} %param.27) | copy-start | bytes 388
  149.2 63.7 %copy-start.4 = (f32[4096,4]{0,1:T(4,128)S(1)}, f32[4096,4]{0,1:T(4,128)}, u32[]{:S(2)}) copy-start(f32[4096,4]{0,1:T(4,128)} %param.23) | copy-start | bytes 196612
  149.2 63.8 %copy-start.5 = (f32[4096]{0:T(1024)S(1)}, f32[4096]{0:T(1024)}, u32[]{:S(2)}) copy-start(f32[4096]{0:T(1024)} %param.22) | copy-start | bytes 49156
  196.8 231.0 %copy-start.3 = (bf16[16,512]{1,0:T(8,128)(2,1)}, bf16[16,512]{1,0:T(8,128)(2,1)S(1)}, u32[]{:S(2)}) copy-start(bf16[16,512]{1,0:T(8,128)(2,1)S(1)} %fusion.16) | copy-start | bytes 49156
  197.5 15.2 %all-to-all-start = ((bf16[8,16,512]{2,1,0:T(8,128)(2,1)}), bf16[8,16,512]{2,1,0:T(8,128)(2,1)S(1)}, u32[]{:S(2)}, u32[]{:S(2)}) async-start(bf16[8,16,512]{2,1,0:T(8,128)(2,1)} %broadcast_in_dim.33), calls=%async_computation | async-start | bytes 262144 | tf_op jit(solution)/shard_map/all_to_all | solution.py:25
  204.7 78.2 %all-gather.9.cloned.1.call-start = ((), (), s32[]{:S(2)}) async-start(), calls=%async_computation.8 | async-start | bytes 4325376 | tf_op jit(solution)/shard_map/all_gather | solution.py:154
  214.6 73.9 %copy-start.1 = (bf16[1,4096,128]{2,1,0:T(8,128)(2,1)S(1)}, bf16[1,4096,128]{2,1,0:T(8,128)(2,1)}, u32[]{:S(2)}) copy-start(bf16[1,4096,128]{2,1,0:T(8,128)(2,1)} %param.24) | copy-start | bytes 3145732
  214.6 114.8 %reduce-scatter.3.cloned.1.call-start = ((), (), s32[]{:S(2)}) async-start(), calls=%async_computation.6 | async-start | bytes 4718592 | tf_op jit(solution)/shard_map/reduce_scatter | solution.py:47
  288.5 3.0 copy-start.2
  309.7 23.5 %copy-start.7 = (bf16[16,128]{1,0:T(8,128)(2,1)S(1)}, bf16[16,128]{1,0:T(8,128)(2,1)}, u32[]{:S(2)}) copy-start(bf16[16,128]{1,0:T(8,128)(2,1)} %param.16) | copy-start | bytes 12292
  309.7 23.5 %copy-start.8 = (bf16[16,128]{1,0:T(8,128)(2,1)S(1)}, bf16[16,128]{1,0:T(8,128)(2,1)}, u32[]{:S(2)}) copy-start(bf16[16,128]{1,0:T(8,128)(2,1)} %param.15) | copy-start | bytes 12292
  309.7 101.4 %reduce-scatter.5.cloned.1.call-start = ((), (), s32[]{:S(2)}) async-start(), calls=%async_computation.7 | async-start | bytes 2228224 | tf_op jit(solution)/shard_map/reduce_scatter | solution.py:47
  412.7 15.1 %all-to-all-start.1 = ((bf16[12,8,512]{2,0,1:T(8,128)(2,1)}), bf16[12,8,512]{2,0,1:T(8,128)(2,1)S(1)}, u32[]{:S(2)}, u32[]{:S(2)}) async-start(bf16[12,8,512]{2,0,1:T(8,128)(2,1)} %copy.53), calls=%async_computation.3 | async-start | bytes 262144 | tf_op jit(solution)/shard_map/all_to_all | solution.py:164
Sparse Core Ops, SparseCore 0:
  10.2 109.7 all-gather.4
  122.1 71.8 all-gather.6
  214.7 68.1 all-gather.8
  309.8 19.6 reduce-scatter.2
  333.3 77.7 reduce-scatter.4
where the time goes:
time: 436 us; the launch traced here: 435 us
  waiting for transfers between devices  310 us (71%)
  blocking collectives  47 us (11%)
  local copies, waits for them, and re-layouts  24.3 us (6%)
  matrix products  18.8 us (4%)
  starting transfers between devices  15.1 us (3%)
  between operations  14.7 us (3%)
  other arithmetic  5.04 us (1%)
    all_gather x1, waiting for transfers between devices, in_one_piece(): lax.all_gather(both, axis, axis=dim, tiled=True)  106 us
    reduce_scatter x2, waiting for transfers between devices, own_block(): tiles = lax.psum_scatter(tiles, axes[k], scatter_dimension=0, tiled=True)  74.4 us
    all_gather x1, waiting for transfers between devices, body(): piece = lax.all_gather(slot_rows, SEQ, axis=0, tiled=True)  68.2 us
    all_gather x1, waiting for transfers between devices, body(): lax.all_gather(out_proj, SEQ, axis=0, tiled=True)  44.8 us
    all_gather x1, blocking collectives, body(): lax.all_gather(attn_local, 'rep', axis=1, tiled=True)  24.7 us
    all_gather x1, blocking collectives, in_one_piece(): lax.all_gather(both, axis, axis=dim, tiled=True)  22.3 us
  transfers between devices with their start and end apart: 7, of which 7 were waited for; matrix products, arithmetic and copies ran while one was open for 2% of the time, Pallas kernels for 0%

commit v1 on v0

--- a/solution.py
+++ b/solution.py
@@ -9,6 +9,11 @@
 CAP = 12
 SEQ = ("seq_0", "seq_1")
 GROUPS_SEQ = ("groups", "seq_0", "seq_1")
+
+
+def tiled_gather(x, axis, dim):
+    copies = jnp.concatenate([x] * lax.axis_size(axis), axis=dim)
+    return lax.all_to_all(copies, axis, dim, dim, tiled=True)
 
 
 def in_one_piece(arrays, axis, dim, along):
@@ -116,7 +121,7 @@
         (numerator / totals[:, None]).reshape(tok_count, q_per * head_dim).astype(jnp.bfloat16)
     )
     attn_full, keys_cache, values_cache = (
-        lax.all_gather(attn_local, "rep", axis=1, tiled=True),
+        tiled_gather(attn_local, "rep", 1),
         *in_one_piece((keys_new, values_new), "rep", 1, 0),
     )
     projected = jnp.dot(

time: 436 us -> 436 us (level)
  waiting for transfers between devices: 310 us -> 320 us
  blocking collectives: 47 us -> 37.4 us
    all_gather x1 -> x0, blocking collectives: 24.7 us -> none  [body(): lax.all_gather(attn_local, 'rep', axis=1, tiled=True)]
    all_to_all x0 -> x1, blocking collectives: none -> 15 us  [tiled_gather(): return lax.all_to_all(copies, axis, dim, dim, tiled=True)]
    all_gather x1, waiting for transfers between devices: 44.8 us -> 54.4 us  [body(): lax.all_gather(out_proj, SEQ, axis=0, tiled=True)]
where the time goes in v1:
time: 436 us; the launch traced here: 435 us
  waiting for transfers between devices  320 us (73%)
  blocking collectives  37.4 us (9%)
  local copies, waits for them, and re-layouts  24.3 us (6%)
  matrix products  18.8 us (4%)
  starting transfers between devices  14.8 us (3%)
  between operations  14.7 us (3%)
  other arithmetic  5.04 us (1%)
    all_gather x1, waiting for transfers between devices, in_one_piece(): lax.all_gather(both, axis, axis=dim, tiled=True)  106 us
    reduce_scatter x2, waiting for transfers between devices, own_block(): tiles = lax.psum_scatter(tiles, axes[k], scatter_dimension=0, tiled=True)  74.7 us
    all_gather x1, waiting for transfers between devices, body(): piece = lax.all_gather(slot_rows, SEQ, axis=0, tiled=True)  68.2 us
    all_gather x1, waiting for transfers between devices, body(): lax.all_gather(out_proj, SEQ, axis=0, tiled=True)  54.4 us
    all_gather x1, blocking collectives, in_one_piece(): lax.all_gather(both, axis, axis=dim, tiled=True)  22.4 us
    all_to_all x1, blocking collectives, tiled_gather(): return lax.all_to_all(copies, axis, dim, dim, tiled=True)  15 us
  transfers between devices with their start and end apart: 7, of which 7 were waited for; matrix products, arithmetic and copies ran while one was open for 2% of the time, Pallas kernels for 0%

profile of v1, /device:TPU:66, one launch (start us, length us, event | category | flops | bytes accessed | tf_op | source)
XLA Modules:
  0.0 435.2 jit_solution(3757974615029496302)
XLA Ops:
  7.2 0.0 copy-start
  7.2 0.1 all-gather.5.cloned.1.call-start
  7.3 1.7 maximum_maximum_fusion
  8.9 0.1 all-gather.5.cloned.1.call-update
  9.0 0.1 all-gather.7.cloned.1.call-start
  9.0 0.7 all-gather.7.cloned.1.call-update
  9.8 0.7 reshape.179
  10.5 1.3 fusion.64
  12.5 0.9 select_reduce_fusion.1
  13.5 106.4 %all-gather.5.cloned.1.call-done = bf16[8704,256]{1,0:T(8,128)(2,1)} async-done(((bf16[272,256]{1,0:T(8,128)(2,1)}), bf16[8704,256]{1,0:T(8,128)(2,1)}) %all-gather.5.cloned.1.call-update) | async-done | bytes 4456464 | tf_op jit(solution)/shard_map/all_gather | solution.py:21
  119.9 2.8 select_reduce_fusion
  122.7 0.9 fusion.5
  123.6 0.8 fusion.22
  124.5 15.0 %all_to_all.30 = bf16[16,8,512]{2,0,1:T(8,128)(2,1)S(1)} all-to-all(bf16[16,8,512]{2,0,1:T(8,128)(2,1)S(1)} %concatenate.19), channel_id=1, replica_groups=mesh['groups'=2,'seq_0'=16,'seq_1'=2,'rep'=8] {'rep'}, dimensions={1} | all-to-all | bytes 262144 | tf_op jit(solution)/shard_map/all_to_all | solution.py:16
  139.6 54.4 %all-gather.7.cloned.1.call-done = bf16[4096,512]{1,0:T(8,128)(2,1)} async-done(((bf16[128,512]{1,0:T(8,128)(2,1)}), bf16[4096,512]{1,0:T(8,128)(2,1)}) %all-gather.7.cloned.1.call-update) | async-done | bytes 4194320 | tf_op jit(solution)/shard_map/all_gather | solution.py:129
  194.0 2.9 fusion.16
  196.9 0.7 broadcast_in_dim.33
  197.5 7.2 %all-to-all-start.1 = ((bf16[8,16,512]{2,1,0:T(8,128)(2,1)}), bf16[8,16,512]{2,1,0:T(8,128)(2,1)S(1)}, u32[]{:S(2)}, u32[]{:S(2)}) async-start(bf16[8,16,512]{2,1,0:T(8,128)(2,1)} %broadcast_in_dim.33), calls=%async_computation.1 | async-start | bytes 262144 | tf_op jit(solution)/shard_map/all_to_all | solution.py:30
  204.8 8.0 %all-to-all-done.1 = bf16[8,16,512]{2,1,0:T(8,128)(2,1)S(1)} async-done(((bf16[8,16,512]{2,1,0:T(8,128)(2,1)}), bf16[8,16,512]{2,1,0:T(8,128)(2,1)S(1)}, u32[]{:S(2)}, u32[]{:S(2)}) %all-to-all-start.1) | async-done | bytes 131104 | tf_op jit(solution)/shard_map/all_to_all | solution.py:30
  212.8 0.1 fusion.32
  213.0 0.3 select_reduce_fusion.2
  213.4 0.1 copy.60
  213.5 0.1 copy.61
  213.6 0.1 fusion.47
  213.7 0.9 fusion.1
  214.6 0.1 all-gather.9.cloned.1.call-update
  214.7 0.0 copy-start.1
  214.7 0.1 reduce-scatter.3.cloned.1.call-start
  214.7 68.2 %all-gather.9.cloned.1.call-done = bf16[32,12,4096]{2,1,0:T(8,128)(2,1)} async-done(((bf16[1,12,4096]{2,1,0:T(8,128)(2,1)}), bf16[32,12,4096]{2,1,0:T(8,128)(2,1)}) %all-gather.9.cloned.1.call-update) | async-done | bytes 3145744 | tf_op jit(solution)/shard_map/all_gather | solution.py:159
  283.0 5.6 %reshape.183 = bf16[384,4096]{1,0:T(8,128)(2,1)} reshape(bf16[32,12,4096]{2,1,0:T(8,128)(2,1)} %all-gather.9.cloned.1.call-done) | data formatting | bytes 6291456
  288.6 2.9 fusion.30
  291.6 7.0 %convolution_convert_fusion = bf16[384,4096]{1,0:T(8,128)(2,1)} fusion(bf16[384,4096]{1,0:T(8,128)(2,1)} %reshape.183, bf16[1,128,4096]{2,1,0:T(8,128)(2,1)S(1)} %copy-done, bf16[1,4096,128]{2,1,0:T(8,128)(2,1)S(1)} %copy-done.2, f32[384,128]{1,0:T(8,128)S(1)} %fusion.30), kind=kOutput, calls=%fused_computation.2 | convolution fusion | flops 807174144 | bytes 8585216 | tf_op jit(solution)/shard_map/dot_general | solution.py:164
  298.6 5.5 %reshape_reshape.3 = bf16[16,2,12,4096]{3,2,1,0:T(8,128)(2,1)} reshape(bf16[384,4096]{1,0:T(8,128)(2,1)} %convolution_convert_fusion) | data formatting | bytes 6291456 | tf_op jit(solution)/shard_map/reshape;reshape | solution.py:48
  304.1 5.6 %copy.63 = bf16[2,16,12,4096]{3,1,0,2:T(8,128)(2,1)} copy(bf16[2,16,12,4096]{3,2,0,1:T(8,128)(2,1)} %bitcast.64) | data formatting | bytes 6291456 | tf_op jit(solution)/shard_map/transpose | solution.py:49
  309.6 0.1 reduce-scatter.3.cloned.1.call-update
  309.7 0.1 reduce-scatter.5.cloned.1.call-start
  309.8 19.7 %reduce-scatter.3.cloned.1.call-done = bf16[16,12,4096]{2,0,1:T(8,128)(2,1)} async-done(((bf16[32,12,4096]{2,0,1:T(8,128)(2,1)}), bf16[16,12,4096]{2,0,1:T(8,128)(2,1)}) %reduce-scatter.3.cloned.1.call-update) | async-done | bytes 1572880 | tf_op jit(solution)/shard_map/reduce_scatter | solution.py:52
  329.5 3.7 copy.64
  333.2 0.1 reduce-scatter.5.cloned.1.call-update
  333.3 22.4 %all_gather.15 = bf16[32,1024]{1,0:T(8,128)(2,1)S(1)} all-gather(bf16[32,128]{1,0:T(8,128)(2,1)S(1)} %pad_maximum_fusion), channel_id=1, replica_groups=mesh['groups'=2,'seq_0'=16,'seq_1'=2,'rep'=8] {'rep'}, dimensions={1}, use_global_device_ids=true | all-gather | bytes 73728 | tf_op jit(solution)/shard_map/all_gather | solution.py:21
  355.6 0.6 fusion.72
  356.3 55.0 %reduce-scatter.5.cloned.1.call-done = bf16[1,12,4096]{2,1,0:T(8,128)(2,1)} async-done(((bf16[16,12,4096]{2,1,0:T(8,128)(2,1)}), bf16[1,12,4096]{2,1,0:T(8,128)(2,1)}) %reduce-scatter.5.cloned.1.call-update) | async-done | bytes 98320 | tf_op jit(solution)/shard_map/reduce_scatter | solution.py:52
  411.2 0.9 copy.70
  412.2 0.7 copy.65
  412.9 7.3 %all-to-all-start.2 = ((bf16[12,8,512]{2,0,1:T(8,128)(2,1)}), bf16[12,8,512]{2,0,1:T(8,128)(2,1)S(1)}, u32[]{:S(2)}, u32[]{:S(2)}) async-start(bf16[12,8,512]{2,0,1:T(8,128)(2,1)} %copy.65), calls=%async_computation.4 | async-start | bytes 262144 | tf_op jit(solution)/shard_map/all_to_all | solution.py:169
  420.2 0.2 convolution_bitcast_fusion
  420.4 7.4 %all-to-all-done.2 = bf16[12,8,512]{2,0,1:T(8,128)(2,1)S(1)} async-done(((bf16[12,8,512]{2,0,1:T(8,128)(2,1)}), bf16[12,8,512]{2,0,1:T(8,128)(2,1)S(1)}, u32[]{:S(2)}, u32[]{:S(2)}) %all-to-all-start.2) | async-done | bytes 98336 | tf_op jit(solution)/shard_map/all_to_all | solution.py:169
  427.8 0.8 fusion.15
  (40 shorter events, 0.3 us)
Async XLA Ops:
  7.2 284.4 %copy-start = (bf16[1,128,4096]{2,1,0:T(8,128)(2,1)S(1)}, bf16[1,128,4096]{2,1,0:T(8,128)(2,1)}, u32[]{:S(2)}) copy-start(bf16[1,128,4096]{2,1,0:T(8,128)(2,1)} %param.26) | copy-start | bytes 3145732
  7.2 112.7 %all-gather.5.cloned.1.call-start = ((), (), s32[]{:S(2)}) async-start(), calls=%async_computation.5 | async-start | bytes 4595712 | tf_op jit(solution)/shard_map/all_gather | solution.py:21
  9.0 185.0 %all-gather.7.cloned.1.call-start = ((), (), s32[]{:S(2)}) async-start(), calls=%async_computation.6 | async-start | bytes 4325376 | tf_op jit(solution)/shard_map/all_gather | solution.py:129
  119.9 3.7 copy-start.10
  123.6 70.4 %copy-start.6 = (bf16[16,512]{1,0:T(8,128)(2,1)S(1)}, bf16[16,512]{1,0:T(8,128)(2,1)}, u32[]{:S(2)}) copy-start(bf16[16,512]{1,0:T(8,128)(2,1)} %param.20) | copy-start | bytes 49156
  194.0 10.8 %copy-start.9 = (s32[16,2]{0,1:T(2,128)S(1)}, s32[16,2]{0,1:T(2,128)}, u32[]{:S(2)}) copy-start(s32[16,2]{0,1:T(2,128)} %param.27) | copy-start | bytes 388
  194.0 19.0 %copy-start.4 = (f32[4096,4]{0,1:T(4,128)S(1)}, f32[4096,4]{0,1:T(4,128)}, u32[]{:S(2)}) copy-start(f32[4096,4]{0,1:T(4,128)} %param.23) | copy-start | bytes 196612
  194.0 19.0 %copy-start.5 = (f32[4096]{0:T(1024)S(1)}, f32[4096]{0:T(1024)}, u32[]{:S(2)}) copy-start(f32[4096]{0:T(1024)} %param.22) | copy-start | bytes 49156
  196.9 230.9 %copy-start.3 = (bf16[16,512]{1,0:T(8,128)(2,1)}, bf16[16,512]{1,0:T(8,128)(2,1)S(1)}, u32[]{:S(2)}) copy-start(bf16[16,512]{1,0:T(8,128)(2,1)S(1)} %fusion.16) | copy-start | bytes 49156
  197.5 15.2 %all-to-all-start.1 = ((bf16[8,16,512]{2,1,0:T(8,128)(2,1)}), bf16[8,16,512]{2,1,0:T(8,128)(2,1)S(1)}, u32[]{:S(2)}, u32[]{:S(2)}) async-start(bf16[8,16,512]{2,1,0:T(8,128)(2,1)} %broadcast_in_dim.33), calls=%async_computation.1 | async-start | bytes 262144 | tf_op jit(solution)/shard_map/all_to_all | solution.py:30
  204.8 78.2 %all-gather.9.cloned.1.call-start = ((), (), s32[]{:S(2)}) async-start(), calls=%async_computation.9 | async-start | bytes 4325376 | tf_op jit(solution)/shard_map/all_gather | solution.py:159
  214.7 73.9 %copy-start.1 = (bf16[1,4096,128]{2,1,0:T(8,128)(2,1)S(1)}, bf16[1,4096,128]{2,1,0:T(8,128)(2,1)}, u32[]{:S(2)}) copy-start(bf16[1,4096,128]{2,1,0:T(8,128)(2,1)} %param.24) | copy-start | bytes 3145732
  214.7 114.8 %reduce-scatter.3.cloned.1.call-start = ((), (), s32[]{:S(2)}) async-start(), calls=%async_computation.7 | async-start | bytes 4718592 | tf_op jit(solution)/shard_map/reduce_scatter | solution.py:52
  288.6 3.0 copy-start.2
  309.7 23.5 %copy-start.7 = (bf16[16,128]{1,0:T(8,128)(2,1)S(1)}, bf16[16,128]{1,0:T(8,128)(2,1)}, u32[]{:S(2)}) copy-start(bf16[16,128]{1,0:T(8,128)(2,1)} %param.16) | copy-start | bytes 12292
  309.7 23.5 %copy-start.8 = (bf16[16,128]{1,0:T(8,128)(2,1)S(1)}, bf16[16,128]{1,0:T(8,128)(2,1)}, u32[]{:S(2)}) copy-start(bf16[16,128]{1,0:T(8,128)(2,1)} %param.15) | copy-start | bytes 12292
  309.7 101.5 %reduce-scatter.5.cloned.1.call-start = ((), (), s32[]{:S(2)}) async-start(), calls=%async_computation.8 | async-start | bytes 2228224 | tf_op jit(solution)/shard_map/reduce_scatter | solution.py:52
  412.9 14.9 %all-to-all-start.2 = ((bf16[12,8,512]{2,0,1:T(8,128)(2,1)}), bf16[12,8,512]{2,0,1:T(8,128)(2,1)S(1)}, u32[]{:S(2)}, u32[]{:S(2)}) async-start(bf16[12,8,512]{2,0,1:T(8,128)(2,1)} %copy.65), calls=%async_computation.4 | async-start | bytes 262144 | tf_op jit(solution)/shard_map/all_to_all | solution.py:169
Sparse Core Ops, SparseCore 0:
  10.2 109.7 all-gather.4
  122.1 71.8 all-gather.6
  214.8 68.1 all-gather.8
  309.8 19.6 reduce-scatter.2
  333.4 77.8 reduce-scatter.4
